TPU v7x, 16 devices: a 4x2x1 block of a 4x4x4 slice. The times are simulated.
16 devices in a mesh: dp: 4 (over y, z, core), tp: 4 (over x).
Axes of the slice: x: 4, y: 2, z: 1, core: 2. Of those that a mesh axis runs over, the one named last changes fastest.
The devices are a block of a 4x4x4 slice.
Arguments:
- x: bfloat16 [256, 2560], P('dp'), parts along dimension 0
- k_cache: bfloat16 [256, 4096, 8, 128], P('dp', None, 'tp'), parts along dimension 0
- v_cache: bfloat16 [256, 4096, 8, 128], P('dp', None, 'tp'), parts along dimension 0
- gain_a: bfloat16 [2560], replicated
- wq: bfloat16 [2560, 4096], P(None, 'tp')
- wo: bfloat16 [4096, 2560], P('tp')
- gain_m: bfloat16 [2560], replicated
- w_gate: bfloat16 [2560, 9728], P(None, 'tp')
- w_up: bfloat16 [2560, 9728], P(None, 'tp')
- w_down: bfloat16 [9728, 2560], P('tp')
Outputs:
- output: bfloat16 [256, 2560], P('dp'), parts along dimension 0
There are 4 independent parts. A program takes and returns all parts, laid end to end along the dimension named above; an argument that names none is the same for every part.
All inputs are finite; a program needn't handle non-finite values.
Results may differ from a plain program's by a relative error of at most 0.017.
Values are sent between devices in bfloat16 or wider.
A program may use at most 1.5 GiB of HBM per device.

v0:
```python
import jax
import jax.numpy as jnp
from jax import lax
from jax.sharding import PartitionSpec as P

HEAD = 128
THETA = 10000


def normed(x, gain):
    wide = x.astype(jnp.float32)
    scale = lax.rsqrt(jnp.mean(wide * wide, -1, keepdims=True) + 1e-6)
    return (wide * scale * gain.astype(jnp.float32)).astype(jnp.bfloat16)


def turned(t, place, theta):
    half = t.shape[-1] // 2
    angle = place.astype(jnp.float32)[:, None] * theta ** (-jnp.arange(half, dtype=jnp.float32) / half)
    cos, sin = jnp.cos(angle)[:, None], jnp.sin(angle)[:, None]
    a, b = t[..., :half].astype(jnp.float32), t[..., half:].astype(jnp.float32)
    return jnp.concatenate([a * cos - b * sin, b * cos + a * sin], -1).astype(jnp.bfloat16)


def matmul(a, w):
    return jnp.dot(a, w, preferred_element_type=jnp.float32).astype(jnp.bfloat16)


def einsum(form, a, b):
    return jnp.einsum(form, a.astype(jnp.float32), b.astype(jnp.float32))


def seen_by(a, wq, k_cache, v_cache, head, theta):
    batch, cache, kv_heads = k_cache.shape[:3]
    place = jnp.full((batch,), cache - 1)
    q = turned(matmul(a, wq).reshape(batch, -1, head), place, theta).reshape(batch, kv_heads, -1, head)
    scores = einsum("bgsd,bugd->bgsu", q, k_cache) * head**-0.5
    weights = jax.nn.softmax(scores, -1).astype(jnp.bfloat16)
    return einsum("bgsu,bugd->bgsd", weights, v_cache).astype(jnp.bfloat16).reshape(batch, -1)


def hidden_of(b, w_gate, w_up):
    gate = jnp.dot(b, w_gate, preferred_element_type=jnp.float32)
    up = jnp.dot(b, w_up, preferred_element_type=jnp.float32)
    return (jax.nn.silu(gate) * up).astype(jnp.bfloat16)


def solution(mesh):
    def added(t, term):
        return (t.astype(jnp.float32) + lax.psum(term.astype(jnp.bfloat16), "tp").astype(jnp.float32)).astype(jnp.bfloat16)

    def step(x, k_cache, v_cache, gain_a, wq, wo, gain_m, w_gate, w_up, w_down):
        seen = seen_by(normed(x, gain_a), wq, k_cache, v_cache, HEAD, THETA)
        h = added(x, jnp.dot(seen, wo, preferred_element_type=jnp.float32))
        return added(h, jnp.dot(hidden_of(normed(h, gain_m), w_gate, w_up), w_down, preferred_element_type=jnp.float32))

    states, cache, columns, rows_of = P("dp", None), P("dp", None, "tp", None), P(None, "tp"), P("tp", None)
    return jax.shard_map(
        step,
        mesh=mesh,
        in_specs=(states, cache, cache, P(None), columns, rows_of, P(None), columns, columns, rows_of),
        out_specs=states,
        check_vma=False,
    )
```

profile of v0, /device:TPU:112, one launch (start us, length us, event | category | flops | bytes accessed | tf_op | source)
XLA Modules:
  0.0 241.5 jit_solution(1696579296723906280)
XLA Ops:
  6.5 0.0 all-reduce.3.cloned.1.call-start
  6.6 0.7 convert_element_type.63
  7.3 1.1 fusion.13
  8.5 3.7 %fusion.12 = bf16[8,8,8,128]{3,1,2,0:T(8,128)(2,1)S(1)} fusion(bf16[2560,1024]{1,0:T(8,128)(2,1)} %param.14, bf16[64,2560]{1,0:T(8,128)(2,1)} %param.10, f32[2560]{0:T(1024)S(1)} %convert_element_type.63, f32[64]{0:T(128)S(1)} %add_rsqrt_fusion.1), kind=kOutput, calls=%fused_computation.17 | convolution fusion | flops 336265216 | bytes 5712128 | tf_op jit(solution)/shard_map/dot_general | solution.py:25
  12.2 0.1 fusion.29
  12.3 62.3 %fusion.3 = f32[64,2,4,4096]{3,2,1,0:T(4,128)} fusion(bf16[64,4096,2,128]{3,2,1,0:T(2,128)(2,1)} %param.11, bf16[64,2,4,64]{3,2,1,0:T(4,128)(2,1)S(1)} %bitcast.13, bf16[64,2,4,64]{3,2,1,0:T(4,128)(2,1)S(1)} %bitcast.12), kind=kOutput, calls=%fused_computation.3 | convolution fusion | flops 537133056 | bytes 142737408 | tf_op jit(solution)/shard_map/bgsd,bugd->bgsu/dot_general | solution.py:29
  74.6 12.9 %fusion.45 = (f32[64,2,4]{2,1,0:T(2,128)S(1)}, f32[64,2,4,4096]{3,2,1,0:T(4,128)}) fusion(f32[64,2,4,4096]{3,2,1,0:T(4,128)} %fusion.3), kind=kOutput, calls=%fused_computation.58 | output fusion | flops 6295551 | bytes 16779264 | tf_op jit(solution)/shard_map/sub | solution.py:37
  87.5 0.0 copy-start.1
  87.5 0.0 copy-start
  87.5 48.3 %fusion.9 = bf16[64,2,4,128]{3,2,1,0:T(4,128)(2,1)S(1)} fusion(bf16[64,4096,2,128]{3,2,1,0:T(2,128)(2,1)} %param.12, f32[64,2,4,4096]{3,2,1,0:T(4,128)} %get-tuple-element.10, f32[64,2,4]{2,1,0:T(2,128)S(1)} %get-tuple-element.9), kind=kOutput, calls=%fused_computation.15 | convolution fusion | flops 541130752 | bytes 142739456 | tf_op jit(solution)/shard_map/bgsu,bugd->bgsd/dot_general | solution.py:29
  135.8 0.1 reshape.40
  135.9 4.2 %convolution_convert_fusion = bf16[64,2560]{1,0:T(8,128)(2,1)} fusion(bf16[64,1024]{1,0:T(8,128)(2,1)S(1)} %reshape.40, bf16[1024,2560]{1,0:T(8,128)(2,1)} %param.15), kind=kOutput, calls=%fused_computation.13 | convolution fusion | flops 335708160 | bytes 5701632 | tf_op jit(solution)/shard_map/dot_general | solution.py:53
  140.1 0.1 all-reduce.3.cloned.1.call-update
  140.2 0.1 all-reduce.5.cloned.1.call-start
  140.3 0.0 copy-done.1
  140.3 36.8 %all-reduce.3.cloned.1.call-done = bf16[64,2560]{1,0:T(8,128)(2,1)} async-done(((bf16[64,2560]{1,0:T(8,128)(2,1)}), bf16[64,2560]{1,0:T(8,128)(2,1)}) %all-reduce.3.cloned.1.call-update) | async-done | bytes 327696 | tf_op jit(solution)/shard_map/psum | solution.py:49
  177.0 0.0 copy-done
  177.0 1.2 fusion.17
  178.2 6.9 %fusion.37 = f32[64,2432]{1,0:T(8,128)S(1)} fusion(bf16[2560,2432]{1,0:T(8,128)(2,1)} %param.17, bf16[64,2560]{1,0:T(8,128)(2,1)S(1)} %get-tuple-element.6, f32[2560]{0:T(1024)S(1)} %convert_element_type.74, f32[64]{0:T(128)S(1)} %add_rsqrt_fusion), kind=kOutput, calls=%fused_computation.49 | convolution fusion | flops 797573120 | bytes 13412608 | tf_op jit(solution)/shard_map/dot_general | solution.py:42
  185.1 13.3 %convolution_convert_fusion.1 = bf16[64,2560]{1,0:T(8,128)(2,1)} fusion(bf16[2432,2560]{1,0:T(8,128)(2,1)} %param.19, bf16[2560,2432]{1,0:T(8,128)(2,1)} %param.18, f32[64,2432]{1,0:T(8,128)S(1)} %fusion.37, bf16[64,2560]{1,0:T(8,128)(2,1)S(1)} %get-tuple-element.6, f32[2560]{0:T(1024)S(1)} %convert_element_type.74, f32[64]{0:T(128)S(1)} %add_rsqrt_fusion), kind=kOutput, calls=%fused_computation.14 | convolution fusion | flops 1595588608 | bytes 26192128 | tf_op jit(solution)/shard_map/dot_general | solution.py:54
  198.4 0.1 all-reduce.5.cloned.1.call-update
  198.4 34.4 %all-reduce.5.cloned.1.call-done = bf16[64,2560]{1,0:T(8,128)(2,1)} async-done(((bf16[64,2560]{1,0:T(8,128)(2,1)}), bf16[64,2560]{1,0:T(8,128)(2,1)}) %all-reduce.5.cloned.1.call-update) | async-done | bytes 327696 | tf_op jit(solution)/shard_map/psum | solution.py:49
  232.8 1.8 fusion.20
  (5 shorter events, 0.1 us)
Async XLA Ops:
  6.5 170.5 %all-reduce.3.cloned.1.call-start = ((), (), s32[]{:S(2)}) async-start(), calls=%async_computation | async-start | bytes 655360 | tf_op jit(solution)/shard_map/psum | solution.py:49
  87.5 52.8 %copy-start.1 = (bf16[2560]{0:T(1024)(128)(2,1)S(1)}, bf16[2560]{0:T(1024)(128)(2,1)}, u32[]{:S(2)}) copy-start(bf16[2560]{0:T(1024)(128)(2,1)} %param.16) | copy-start | bytes 15364
  87.5 89.5 %copy-start = (bf16[64,2560]{1,0:T(8,128)(2,1)S(1)}, bf16[64,2560]{1,0:T(8,128)(2,1)}, u32[]{:S(2)}) copy-start(bf16[64,2560]{1,0:T(8,128)(2,1)} %param.10) | copy-start | bytes 983044
  140.2 92.7 %all-reduce.5.cloned.1.call-start = ((), (), s32[]{:S(2)}) async-start(), calls=%async_computation.1 | async-start | bytes 655360 | tf_op jit(solution)/shard_map/psum | solution.py:49
Sparse Core Ops, SparseCore 0:
  140.3 36.6 all-reduce.2
  198.6 34.2 all-reduce.4
where the time goes:
time: 242 us; the launch traced here: 241 us
  matrix products  139 us (57%)
  waiting for transfers between devices  71.3 us (29%)
  other arithmetic  17.9 us (7%)
  between operations  13.5 us (6%)
    dot_general x2, matrix products, einsum(): return jnp.einsum(form, a.astype(jnp.float32), b.astype(jnp.float32))  111 us
    psum x2, waiting for transfers between devices, added(): lax.psum(term.astype(jnp.bfloat16), 'tp').astype(jnp.float32)  71.2 us
    dot_general x1, matrix products, step(): jnp.dot(hidden_of(normed(h, gain_m), w_gate, w_up), w_down, preferred_ele...  13.3 us
    sub x1, other arithmetic, seen_by(): weights = jax.nn.softmax(scores, -1).astype(jnp.bfloat16)  12.9 us
    dot_general x1, matrix products, hidden_of(): gate = jnp.dot(b, w_gate, preferred_element_type=jnp.float32)  6.87 us
  transfers between devices with their start and end apart: 2, of which 2 were waited for; matrix products, arithmetic and copies ran while one was open for 0% of the time, Pallas kernels for 0%

commit v1 on v0

v1 whole, which is shorter than its diff:
```python
import functools

import jax
import jax.numpy as jnp
import numpy as np
from jax import lax
from jax.experimental import pallas as pl
from jax.experimental.pallas import tpu as pltpu
from jax.sharding import PartitionSpec as P

HEAD = 128
THETA = 10000
DEPTH = 4
TILE = 256
LANES = 128
MESH = pl.DeviceIdType.MESH
F32, BF16 = jnp.float32, jnp.bfloat16
EPS = 1e-6


def dot(a, b):
    return jnp.dot(a, b, preferred_element_type=F32)


def rope_rows(place, head):
    half = head // 2
    angle = place * float(THETA) ** (-np.arange(half, dtype=np.float64) / half)
    cos, sin = np.cos(angle), np.sin(angle)
    return np.stack([np.concatenate([cos, cos]), np.concatenate([-sin, sin])]).astype(np.float32)


def pieces_of(width, step):
    return [(at, min(step, width - at)) for at in range(0, width, step)]


def layer_kernel(
    n, chunks, hidden_pieces, q_pieces,
    x_hbm, k_hbm, v_hbm, gain_a_hbm, gain_m_hbm, rope_hbm, wq_hbm, wo_hbm, wg_hbm, wu_hbm, wd_hbm, out_hbm,
    x_ref, gain_a_ref, gain_m_ref, rope_ref, kbuf, vbuf, wo_ref, wg_refs, wu_refs, wd_ref,
    b_ref, q_ref, seen_ref, s_a, s_b, h_ref, hid_ref, term_refs, rs_send, rs_recv, y_ref,
    x_sem, aux_sem, k_sem, v_sem, wq_sem, wo_sem, wg_sem, wu_sem, wd_sem, out_sem,
    t_send, t_recv, r_send, r_recv, g_send, g_recv,
):
    me = lax.axis_index("tp")
    batch, d = x_ref.shape
    heads = q_ref.shape[0] // batch
    span = kbuf.shape[2]
    block = wd_ref.shape[2]
    peer = [lax.rem(me + s, n) for s in range(n)]

    def copy_k(i):
        slot = lax.rem(i, DEPTH)
        return pltpu.make_async_copy(k_hbm.at[i], kbuf.at[slot], k_sem.at[slot])

    def copy_v(i):
        slot = lax.rem(i, DEPTH)
        return pltpu.make_async_copy(v_hbm.at[i], vbuf.at[slot], v_sem.at[slot])

    copy_x = pltpu.make_async_copy(x_hbm, x_ref, x_sem)
    copies_aux = [
        pltpu.make_async_copy(a, b, aux_sem.at[j])
        for j, (a, b) in enumerate(((gain_a_hbm, gain_a_ref), (gain_m_hbm, gain_m_ref), (rope_hbm, rope_ref)))
    ]
    copy_wo = pltpu.make_async_copy(wo_hbm, wo_ref, wo_sem)
    copies_wq = [
        pltpu.make_async_copy(wq_hbm.at[:, pl.ds(at, w)], wg_refs[j], wq_sem.at[j]) for j, (at, w) in enumerate(q_pieces)
    ]
    copies_wg = [
        pltpu.make_async_copy(wg_hbm.at[:, pl.ds(at, w)], wg_refs[j], wg_sem.at[j]) for j, (at, w) in enumerate(hidden_pieces)
    ]
    copies_wu = [
        pltpu.make_async_copy(wu_hbm.at[:, pl.ds(at, w)], wu_refs[j], wu_sem.at[j]) for j, (at, w) in enumerate(hidden_pieces)
    ]
    order = [2, 1, 3, 0]
    copies_wd = [
        pltpu.make_async_copy(
            wd_hbm.at[:, pl.ds(pl.multiple_of(peer[s] * block, LANES), block)], wd_ref.at[j], wd_sem.at[j]
        )
        for j, s in enumerate(order)
    ]

    copy_x.start()
    for c in copies_aux:
        c.start()
    for c in copies_wq:
        c.start()
    barrier = pltpu.get_barrier_semaphore()
    for s in range(1, n):
        pl.semaphore_signal(barrier, inc=1, device_id={"tp": peer[s]}, device_id_type=MESH)

    def normed(wide, gain):
        scale = lax.rsqrt(jnp.mean(wide * wide, -1, keepdims=True) + EPS)
        return (wide * scale * gain).astype(BF16)

    copy_x.wait()
    for c in copies_aux:
        c.wait()
    for i in range(DEPTH):
        copy_k(i).start()
        copy_v(i).start()
    copy_wo.start()
    gain_a = gain_a_ref[...].astype(F32).reshape(1, d)
    gain_m = gain_m_ref[...].astype(F32).reshape(1, d)
    for r in range(0, batch, 16):
        b_ref[r : r + 16, :] = normed(x_ref[r : r + 16, :].astype(F32), gain_a)
    cos, sin = rope_ref[0:1, :], rope_ref[1:2, :]
    for j, (at, w) in enumerate(q_pieces):
        copies_wq[j].wait()
        part = dot(b_ref[...], wg_refs[j][...]).astype(BF16).astype(F32)
        for c in range(0, w, HEAD):
            t = part[:, c : c + HEAD]
            t = t * cos + pltpu.roll(t, HEAD // 2, 1) * sin
            q_ref[pl.ds((at + c) // HEAD, batch, stride=heads), :] = t.astype(BF16).astype(F32)

    row = lax.broadcasted_iota(jnp.int32, (2 * heads, TILE), 0)
    lane = lax.broadcasted_iota(jnp.int32, (2 * heads, TILE), 1)
    valid = (lane % 2) == ((row % heads) // (heads // 2))
    factor = HEAD**-0.5 * float(np.log2(np.e))
    tiles = range(0, span, TILE)

    def scores(i, s_ref):
        slot = lax.rem(i, DEPTH)
        q = q_ref[pl.ds(pl.multiple_of(i * heads, heads), heads), :]
        zero = jnp.zeros_like(q)
        lhs = jnp.concatenate([jnp.concatenate([q, zero], 1), jnp.concatenate([zero, q], 1)], 0).astype(BF16)
        for t in tiles:
            both = jnp.concatenate([kbuf[slot, 0, t : t + TILE, :], kbuf[slot, 1, t : t + TILE, :]], 1)
            s_ref[:, t : t + TILE] = lax.dot_general(lhs, both, (((1,), (1,)), ((), ())), preferred_element_type=F32)

    def paired(rows, op):
        both = op(rows[:heads], rows[heads:])
        return jnp.concatenate([both, both], 0)

    def attend(i, s_ref):
        slot = lax.rem(i, DEPTH)
        top = s_ref[:, :TILE]
        for t in tiles[1:]:
            top = jnp.maximum(top, s_ref[:, t : t + TILE])
        top = jnp.max(jnp.where(valid, top, -jnp.inf), 1, keepdims=True)
        top = jnp.where(valid, paired(top, jnp.maximum), jnp.inf)
        total = jnp.zeros((2 * heads, TILE), F32)
        for t in tiles:
            e = jnp.exp2((s_ref[:, t : t + TILE] - top) * factor)
            s_ref[:, t : t + TILE] = e
            total = total + e
        inverse = 1.0 / paired(jnp.sum(total, 1, keepdims=True), jnp.add)
        parts = [None, None]
        for c, t in enumerate(tiles):
            weights = (s_ref[:, t : t + TILE] * inverse).astype(BF16)
            both = jnp.concatenate([vbuf[slot, 0, t : t + TILE, :], vbuf[slot, 1, t : t + TILE, :]], 1)
            r = dot(weights, both)
            parts[c % 2] = r if parts[c % 2] is None else parts[c % 2] + r
        r = parts[0] + parts[1]
        seen_ref[pl.ds(pl.multiple_of(i * heads, heads), heads), :] = r[:heads, :HEAD] + r[heads:, HEAD:]

    def refill(copy, i):
        @pl.when(i < batch)
        def _():
            copy(i).start()

    def pair(i):
        copy_k(i + 1).wait()
        copy_v(i).wait()
        scores(i + 1, s_b)
        attend(i, s_a)
        refill(copy_v, i + DEPTH)
        refill(copy_k, i + 1 + DEPTH)
        copy_k(i + 2).wait()
        copy_v(i + 1).wait()
        scores(i + 2, s_a)
        attend(i + 1, s_b)
        refill(copy_v, i + 1 + DEPTH)
        refill(copy_k, i + 2 + DEPTH)

    def send_term(c, s):
        return pltpu.make_async_remote_copy(
            src_ref=term_refs[c].at[me], dst_ref=term_refs[c].at[me], send_sem=t_send.at[c, s - 1], recv_sem=t_recv.at[c, s - 1],
            device_id={"tp": peer[s]}, device_id_type=MESH,
        )

    def project(c, first, count):
        seen = jnp.concatenate(
            [seen_ref[pl.ds(first * heads + g, count, stride=heads), :] for g in range(heads)], 1
        ).astype(BF16)
        for at, w in pieces_of(d, 512):
            term_refs[c][me, :, at : at + w] = dot(seen, wo_ref[:, at : at + w]).astype(BF16)
        for s in (2, 1, 3):
            send_term(c, s).start()

    last_start = batch - 2 - DEPTH

    def start_weights():
        for g, u in zip(copies_wg, copies_wu):
            g.start(priority=1)
            u.start(priority=1)
        for c in copies_wd:
            c.start(priority=1)

    copy_k(0).wait()
    scores(0, s_a)
    copy_k(DEPTH).start()
    for c, (first, count) in enumerate(chunks):
        final = c == len(chunks) - 1

        @pl.loop(0, count // 2 - (1 if final else 0))
        def _(j):
            i = first + 2 * j
            pair(i)

            if final:
                @pl.when(i == last_start)
                def _():
                    start_weights()

        if final:
            i = batch - 2
            copy_k(i + 1).wait()
            copy_v(i).wait()
            scores(i + 1, s_b)
            attend(i, s_a)
            copy_v(i + 1).wait()
            attend(i + 1, s_b)
        if c == 0:
            copy_wo.wait()
            pl.semaphore_wait(barrier, n - 1)
        project(c, first, count)

    for c, (first, count) in enumerate(chunks):
        for s in range(1, n):
            send_term(c, s).wait_recv()
        for r in range(0, count, 16):
            total = term_refs[c][0, r : r + 16, :].astype(F32)
            for s in range(1, n):
                total = total + term_refs[c][s, r : r + 16, :].astype(F32)
            at = first + r
            h = (x_ref[at : at + 16, :].astype(F32) + total).astype(BF16)
            h_ref[at : at + 16, :] = h
            b_ref[at : at + 16, :] = normed(h.astype(F32), gain_m)

    for j, (at, w) in enumerate(hidden_pieces):
        copies_wg[j].wait()
        gate = dot(b_ref[...], wg_refs[j][...])
        copies_wu[j].wait()
        up = dot(b_ref[...], wu_refs[j][...])
        hid_ref[:, at : at + w] = (gate / (1.0 + jnp.exp(-gate)) * up).astype(BF16)

    def send_block(j):
        return pltpu.make_async_remote_copy(
            src_ref=rs_send.at[j], dst_ref=rs_recv.at[j], send_sem=r_send.at[j], recv_sem=r_recv.at[j],
            device_id={"tp": peer[order[j]]}, device_id_type=MESH,
        )

    for j in range(n - 1):
        copies_wd[j].wait()
        rs_send[j] = dot(hid_ref[...], wd_ref[j]).astype(BF16)
        send_block(j).start()
    copies_wd[n - 1].wait()
    total = dot(hid_ref[...], wd_ref[n - 1])
    total = total + h_ref[:, pl.ds(pl.multiple_of(me * block, LANES), block)].astype(F32)
    for j in (1, 2, 0):
        send_block(j).wait_recv()
        total = total + rs_recv[j].astype(F32)
    y_ref[me] = total.astype(BF16)

    def send_done(s):
        return pltpu.make_async_remote_copy(
            src_ref=y_ref.at[me], dst_ref=y_ref.at[me], send_sem=g_send.at[s - 1], recv_sem=g_recv.at[s - 1],
            device_id={"tp": peer[s]}, device_id_type=MESH,
        )

    def write(s):
        owner = peer[(n - s) % n]
        return pltpu.make_async_copy(
            y_ref.at[owner], out_hbm.at[:, pl.ds(pl.multiple_of(owner * block, LANES), block)], out_sem.at[s]
        )

    for s in (2, 1, 3):
        send_done(s).start()
    write(0).start()
    for s in (1, 3, 2):
        send_done(s).wait_recv()
        write(s).start()
    for c in range(len(chunks)):
        for s in range(1, n):
            send_term(c, s).wait_send()
    for j in range(n - 1):
        send_block(j).wait_send()
    for s in range(1, n):
        send_done(s).wait_send()
    for s in range(n):
        write(s).wait()


def solution(mesh):
    n = mesh.shape["tp"]

    def step(x, k_cache, v_cache, gain_a, wq, wo, gain_m, w_gate, w_up, w_down):
        batch, cache, kv_heads, head = k_cache.shape
        d = x.shape[1]
        hidden = w_gate.shape[1]
        heads = wq.shape[1] // head
        span = cache * kv_heads // 2
        k = k_cache.reshape(batch, 2, span, head)
        v = v_cache.reshape(batch, 2, span, head)
        chunks = [(0, batch // 2), (batch // 2, batch // 4), (3 * batch // 4, batch // 4)]
        hidden_pieces = pieces_of(hidden, 512)
        q_pieces = pieces_of(wq.shape[1], 512)
        block = d // n
        dma = pltpu.SemaphoreType.DMA
        any_space = pl.BlockSpec(memory_space=pl.ANY)
        scratch = [
            pltpu.VMEM((batch, d), BF16),
            pltpu.VMEM((d,), BF16),
            pltpu.VMEM((d,), BF16),
            pltpu.VMEM((2, head), F32),
            pltpu.VMEM((DEPTH, 2, span, head), BF16),
            pltpu.VMEM((DEPTH, 2, span, head), BF16),
            pltpu.VMEM(wo.shape, BF16),
            [pltpu.VMEM((d, w), BF16) for _, w in hidden_pieces],
            [pltpu.VMEM((d, w), BF16) for _, w in hidden_pieces],
            pltpu.VMEM((n, hidden, block), BF16),
            pltpu.VMEM((batch, d), BF16),
            pltpu.VMEM((batch * heads, head), F32),
            pltpu.VMEM((batch * heads, head), F32),
            pltpu.VMEM((2 * heads, span), F32),
            pltpu.VMEM((2 * heads, span), F32),
            pltpu.VMEM((batch, d), BF16),
            pltpu.VMEM((batch, hidden), BF16),
            [pltpu.VMEM((n, count, d), BF16) for _, count in chunks],
            pltpu.VMEM((n - 1, batch, block), BF16),
            pltpu.VMEM((n - 1, batch, block), BF16),
            pltpu.VMEM((n, batch, block), BF16),
            dma(()), dma((3,)), dma((DEPTH,)), dma((DEPTH,)), dma((len(q_pieces),)), dma(()),
            dma((len(hidden_pieces),)), dma((len(hidden_pieces),)), dma((n,)), dma((n,)),
            dma((len(chunks), n - 1)), dma((len(chunks), n - 1)), dma((n - 1,)), dma((n - 1,)), dma((n - 1,)), dma((n - 1,)),
        ]
        return pl.pallas_call(
            functools.partial(layer_kernel, n, chunks, hidden_pieces, q_pieces),
            out_shape=jax.ShapeDtypeStruct(x.shape, x.dtype),
            in_specs=[any_space] * 11,
            out_specs=any_space,
            scratch_shapes=scratch,
            compiler_params=pltpu.CompilerParams(collective_id=0, has_side_effects=True, vmem_limit_bytes=67043328),
            name="layer",
        )(x, k, v, gain_a, gain_m, jnp.asarray(rope_rows(cache - 1, head)), wq, wo, w_gate, w_up, w_down)

    states, cache, columns, rows_of = P("dp", None), P("dp", None, "tp", None), P(None, "tp"), P("tp", None)
    return jax.shard_map(
        step,
        mesh=mesh,
        in_specs=(states, cache, cache, P(None), columns, rows_of, P(None), columns, columns, rows_of),
        out_specs=states,
        check_vma=False,
    )
```

time: 242 us -> 112 us (0.46)
  matrix products: 139 us -> 0 us
  Pallas kernels: 0 us -> 110 us
  waiting for transfers between devices: 71.3 us -> 0 us
  other arithmetic: 17.9 us -> 0 us
  between operations: 13.5 us -> 0.01 us
    dot_general x6 -> x0, matrix products: 139 us -> none  [the longest x2 111 us: einsum(): return jnp.einsum(form, a.astype(jnp.float32), b.astype(jnp.float32))]
    pallas_call x0 -> x1, Pallas kernels: none -> 110 us  [step(): pl.pallas_call(functools.partial(layer_kernel, n, chunks, hidden_pieces,...]
    psum x2 -> x0, waiting for transfers between devices: 71.2 us -> none  [added(): lax.psum(term.astype(jnp.bfloat16), 'tp').astype(jnp.float32)]
    sub x1 -> x0, other arithmetic: 12.9 us -> none  [seen_by(): weights = jax.nn.softmax(scores, -1).astype(jnp.bfloat16)]
    convert_element_type x3 -> x0, other arithmetic: 2.48 us -> none  [the longest x1 1.77 us: added(): (t.astype(jnp.float32) + lax.psum(term.astype(jnp.bfloat16), 'tp').astype...]
  transfers between devices with their start and end apart: 2 -> 0, of which waited for: 2 -> 0; matrix products, arithmetic and copies ran while one was open for 0% -> 0% of each run, Pallas kernels for 0% -> 0%
where the time goes in v1:
time: 112 us
  Pallas kernels  110 us (98%)
  local copies, waits for them, and re-layouts  1.72 us (2%)
    pallas_call x1, Pallas kernels, step(): pl.pallas_call(functools.partial(layer_kernel, n, chunks, hidden_pieces,...  110 us

profile of v1, /device:TPU:112, one launch (start us, length us, event | category | flops | bytes accessed | tf_op | source)
XLA Modules:
  0.0 111.9 jit_solution(10431374808855988063)
XLA Ops:
  0.0 110.2 %layer.1 = bf16[64,2560]{1,0:T(8,128)(2,1)} custom-call(bf16[64,2560]{1,0:T(8,128)(2,1)} %x_hbm.1, bf16[64,2,4096,128]{3,2,1,0:T(8,128)(2,1)} %bitcast.k_hbm, bf16[64,2,4096,128]{3,2,1,0:T(8,128)(2,1)} %bitcast.1.v_hbm, bf16[2560]{0:T(1024)(128)(2,1)} %gain_a_hbm.1, bf16[2560]{0:T(1024)(128)(2,1)} %gain_m_hbm.1, f32[2,128]{1,0:T(2,128)} %constant.2.clone.rope_hbm, ...), custom_call_target="tpu_custom_call" | custom-call | tf_op jit(solution)/shard_map/layer/pallas_call | solution.py:337
  110.2 1.7 %copy.13 = bf16[64,2560]{1,0:T(8,128)(2,1)} copy(bf16[64,2560]{1,0:T(8,128)(2,1)} %layer.1) | data formatting | bytes 655360

commit v2 on v1

--- a/solution.py
+++ b/solution.py
@@ -13,6 +13,7 @@
 DEPTH = 4
 TILE = 256
 LANES = 128
+VMEM_BYTES = 67043328
 MESH = pl.DeviceIdType.MESH
 F32, BF16 = jnp.float32, jnp.bfloat16
 EPS = 1e-6
@@ -34,10 +35,10 @@
 
 
 def layer_kernel(
-    n, chunks, hidden_pieces, q_pieces,
+    n, chunks, hidden_pieces, q_pieces, out_pieces,
     x_hbm, k_hbm, v_hbm, gain_a_hbm, gain_m_hbm, rope_hbm, wq_hbm, wo_hbm, wg_hbm, wu_hbm, wd_hbm, out_hbm,
-    x_ref, gain_a_ref, gain_m_ref, rope_ref, kbuf, vbuf, wo_ref, wg_refs, wu_refs, wd_ref,
-    b_ref, q_ref, seen_ref, s_a, s_b, h_ref, hid_ref, term_refs, rs_send, rs_recv, y_ref,
+    x_ref, gain_a_ref, gain_m_ref, rope_ref, kbuf, vbuf, wo_ref, wg_refs, wu_refs, wd_refs,
+    b_ref, q_ref, seen_ref, s_a, s_b, h_ref, hid_ref, term_refs, own_refs, rs_send, rs_recv, y_refs,
     x_sem, aux_sem, k_sem, v_sem, wq_sem, wo_sem, wg_sem, wu_sem, wd_sem, out_sem,
     t_send, t_recv, r_send, r_recv, g_send, g_recv,
 ):
@@ -45,7 +46,6 @@
     batch, d = x_ref.shape
     heads = q_ref.shape[0] // batch
     span = kbuf.shape[2]
-    block = wd_ref.shape[2]
     peer = [lax.rem(me + s, n) for s in range(n)]
 
     def copy_k(i):
@@ -71,12 +71,8 @@
     copies_wu = [
         pltpu.make_async_copy(wu_hbm.at[:, pl.ds(at, w)], wu_refs[j], wu_sem.at[j]) for j, (at, w) in enumerate(hidden_pieces)
     ]
-    order = [2, 1, 3, 0]
     copies_wd = [
-        pltpu.make_async_copy(
-            wd_hbm.at[:, pl.ds(pl.multiple_of(peer[s] * block, LANES), block)], wd_ref.at[j], wd_sem.at[j]
-        )
-        for j, s in enumerate(order)
+        pltpu.make_async_copy(wd_hbm.at[:, pl.ds(at, w)], wd_refs[p], wd_sem.at[p]) for p, (at, w) in enumerate(out_pieces)
     ]
 
     copy_x.start()
@@ -131,7 +127,7 @@
         both = op(rows[:heads], rows[heads:])
         return jnp.concatenate([both, both], 0)
 
-    def attend(i, s_ref):
+    def attend(i, s_ref, ready=None):
         slot = lax.rem(i, DEPTH)
         top = s_ref[:, :TILE]
         for t in tiles[1:]:
@@ -144,6 +140,8 @@
             s_ref[:, t : t + TILE] = e
             total = total + e
         inverse = 1.0 / paired(jnp.sum(total, 1, keepdims=True), jnp.add)
+        if ready is not None:
+            ready.wait()
         parts = [None, None]
         for c, t in enumerate(tiles):
             weights = (s_ref[:, t : t + TILE] * inverse).astype(BF16)
@@ -172,9 +170,13 @@
         refill(copy_v, i + 1 + DEPTH)
         refill(copy_k, i + 2 + DEPTH)
 
+    def landed(ref, sem):
+        return pltpu.make_async_copy(ref, ref, sem)
+
     def send_term(c, s):
+        mine = term_refs[c].at[me]
         return pltpu.make_async_remote_copy(
-            src_ref=term_refs[c].at[me], dst_ref=term_refs[c].at[me], send_sem=t_send.at[c, s - 1], recv_sem=t_recv.at[c, s - 1],
+            src_ref=mine, dst_ref=mine, send_sem=t_send.at[c], recv_sem=t_recv.at[c],
             device_id={"tp": peer[s]}, device_id_type=MESH,
         )
 
@@ -182,19 +184,16 @@
         seen = jnp.concatenate(
             [seen_ref[pl.ds(first * heads + g, count, stride=heads), :] for g in range(heads)], 1
         ).astype(BF16)
-        for at, w in pieces_of(d, 512):
+        for at, w in out_pieces:
             term_refs[c][me, :, at : at + w] = dot(seen, wo_ref[:, at : at + w]).astype(BF16)
         for s in (2, 1, 3):
             send_term(c, s).start()
 
-    last_start = batch - 2 - DEPTH
-
-    def start_weights():
-        for g, u in zip(copies_wg, copies_wu):
-            g.start(priority=1)
-            u.start(priority=1)
-        for c in copies_wd:
-            c.start(priority=1)
+    streamed = [c for pair_of in zip(copies_wg, copies_wu) for c in pair_of] + copies_wd
+
+    def stream(first, count):
+        for c in streamed[first : first + count]:
+            c.start()
 
     copy_k(0).wait()
     scores(0, s_a)
@@ -208,9 +207,13 @@
             pair(i)
 
             if final:
-                @pl.when(i == last_start)
+                @pl.when(i == batch - 6)
                 def _():
-                    start_weights()
+                    stream(0, 1)
+
+                @pl.when(i == batch - 4)
+                def _():
+                    stream(1, 4)
 
         if final:
             i = batch - 2
@@ -218,77 +221,85 @@
             copy_v(i).wait()
             scores(i + 1, s_b)
             attend(i, s_a)
-            copy_v(i + 1).wait()
-            attend(i + 1, s_b)
+            stream(5, 2)
+            attend(i + 1, s_b, copy_v(i + 1))
+            stream(7, 2)
         if c == 0:
             copy_wo.wait()
             pl.semaphore_wait(barrier, n - 1)
         project(c, first, count)
 
+    ahead = len(streamed) - 9
+    out_groups = [(0, 1), (2, 3, 4)]
+    for j in range(ahead):
+        streamed[j].wait()
+        stream(9 + j, 1)
+
     for c, (first, count) in enumerate(chunks):
-        for s in range(1, n):
-            send_term(c, s).wait_recv()
-        for r in range(0, count, 16):
-            total = term_refs[c][0, r : r + 16, :].astype(F32)
+        landed(term_refs[c].at[pl.ds(0, n - 1)], t_recv.at[c]).wait()
+        for r in range(0, count, 8):
+            total = term_refs[c][0, r : r + 8, :].astype(F32)
             for s in range(1, n):
-                total = total + term_refs[c][s, r : r + 16, :].astype(F32)
+                total = total + term_refs[c][s, r : r + 8, :].astype(F32)
             at = first + r
-            h = (x_ref[at : at + 16, :].astype(F32) + total).astype(BF16)
-            h_ref[at : at + 16, :] = h
-            b_ref[at : at + 16, :] = normed(h.astype(F32), gain_m)
-
-    for j, (at, w) in enumerate(hidden_pieces):
-        copies_wg[j].wait()
-        gate = dot(b_ref[...], wg_refs[j][...])
-        copies_wu[j].wait()
-        up = dot(b_ref[...], wu_refs[j][...])
-        hid_ref[:, at : at + w] = (gate / (1.0 + jnp.exp(-gate)) * up).astype(BF16)
-
-    def send_block(j):
+            h = (x_ref[at : at + 8, :].astype(F32) + total).astype(BF16)
+            h_ref[at : at + 8, :] = h
+            b_ref[at : at + 8, :] = normed(h.astype(F32), gain_m)
+
+    for start, upto in ((0, 3), (3, len(hidden_pieces))):
+        for c in streamed[max(ahead, 2 * start) : 2 * upto]:
+            c.wait()
+        for j, (at, w) in list(enumerate(hidden_pieces))[start:upto]:
+            gate = dot(b_ref[...], wg_refs[j][...])
+            up = dot(b_ref[...], wu_refs[j][...])
+            hid_ref[:, at : at + w] = (gate / (1.0 + jnp.exp(-gate)) * up).astype(BF16)
+
+    def share(at, w):
+        return pl.ds(pl.multiple_of(at + me * (w // n), LANES), w // n)
+
+    def send_part(p, s):
         return pltpu.make_async_remote_copy(
-            src_ref=rs_send.at[j], dst_ref=rs_recv.at[j], send_sem=r_send.at[j], recv_sem=r_recv.at[j],
-            device_id={"tp": peer[order[j]]}, device_id_type=MESH,
-        )
-
-    for j in range(n - 1):
-        copies_wd[j].wait()
-        rs_send[j] = dot(hid_ref[...], wd_ref[j]).astype(BF16)
-        send_block(j).start()
-    copies_wd[n - 1].wait()
-    total = dot(hid_ref[...], wd_ref[n - 1])
-    total = total + h_ref[:, pl.ds(pl.multiple_of(me * block, LANES), block)].astype(F32)
-    for j in (1, 2, 0):
-        send_block(j).wait_recv()
-        total = total + rs_recv[j].astype(F32)
-    y_ref[me] = total.astype(BF16)
-
-    def send_done(s):
-        return pltpu.make_async_remote_copy(
-            src_ref=y_ref.at[me], dst_ref=y_ref.at[me], send_sem=g_send.at[s - 1], recv_sem=g_recv.at[s - 1],
+            src_ref=rs_send[p].at[peer[s]], dst_ref=rs_recv[p].at[s - 1], send_sem=r_send, recv_sem=r_recv.at[p],
             device_id={"tp": peer[s]}, device_id_type=MESH,
         )
 
-    def write(s):
-        owner = peer[(n - s) % n]
-        return pltpu.make_async_copy(
-            y_ref.at[owner], out_hbm.at[:, pl.ds(pl.multiple_of(owner * block, LANES), block)], out_sem.at[s]
+    def send_done(p, s):
+        mine = y_refs[p].at[:, share(0, out_pieces[p][1])]
+        return pltpu.make_async_remote_copy(
+            src_ref=mine, dst_ref=mine, send_sem=g_send, recv_sem=g_recv.at[p], device_id={"tp": peer[s]}, device_id_type=MESH,
         )
 
-    for s in (2, 1, 3):
-        send_done(s).start()
-    write(0).start()
-    for s in (1, 3, 2):
-        send_done(s).wait_recv()
-        write(s).start()
+    def write(p):
+        at, w = out_pieces[p]
+        return pltpu.make_async_copy(y_refs[p], out_hbm.at[:, pl.ds(at, w)], out_sem)
+
+    for group in out_groups:
+        for p in group:
+            copies_wd[p].wait()
+        for p in group:
+            term = dot(hid_ref[...], wd_refs[p][...])
+            own_refs[p][...] = term
+            width = out_pieces[p][1] // n
+            for j in range(n):
+                rs_send[p][j] = term[:, j * width : (j + 1) * width].astype(BF16)
+            for s in (2, 1, 3):
+                send_part(p, s).start()
+    for p, (at, w) in enumerate(out_pieces):
+        landed(rs_recv[p], r_recv.at[p]).wait()
+        total = own_refs[p][:, share(0, w)]
+        for s in range(1, n):
+            total = total + rs_recv[p][s - 1].astype(F32)
+        y_refs[p][:, share(0, w)] = (h_ref[:, share(at, w)].astype(F32) + total).astype(BF16)
+        for s in (2, 1, 3):
+            send_done(p, s).start()
+    for p, (at, w) in enumerate(out_pieces):
+        landed(y_refs[p].at[:, pl.ds(0, w - w // n)], g_recv.at[p]).wait()
+        write(p).start()
     for c in range(len(chunks)):
-        for s in range(1, n):
-            send_term(c, s).wait_send()
-    for j in range(n - 1):
-        send_block(j).wait_send()
-    for s in range(1, n):
-        send_done(s).wait_send()
-    for s in range(n):
-        write(s).wait()
+        landed(term_refs[c].at[pl.ds(0, n - 1)], t_send.at[c]).wait()
+    for sem in (r_send, g_send):
+        landed(h_ref.at[:, pl.ds(0, d - d // n)], sem).wait()
+    landed(h_ref, out_sem).wait()
 
 
 def solution(mesh):
@@ -302,10 +313,11 @@
         span = cache * kv_heads // 2
         k = k_cache.reshape(batch, 2, span, head)
         v = v_cache.reshape(batch, 2, span, head)
-        chunks = [(0, batch // 2), (batch // 2, batch // 4), (3 * batch // 4, batch // 4)]
+        last = 8
+        chunks = [(0, batch // 2), (batch // 2, batch // 2 - last), (batch - last, last)]
         hidden_pieces = pieces_of(hidden, 512)
         q_pieces = pieces_of(wq.shape[1], 512)
-        block = d // n
+        out_pieces = pieces_of(d, 512)
         dma = pltpu.SemaphoreType.DMA
         any_space = pl.BlockSpec(memory_space=pl.ANY)
         scratch = [
@@ -318,7 +330,7 @@
             pltpu.VMEM(wo.shape, BF16),
             [pltpu.VMEM((d, w), BF16) for _, w in hidden_pieces],
             [pltpu.VMEM((d, w), BF16) for _, w in hidden_pieces],
-            pltpu.VMEM((n, hidden, block), BF16),
+            [pltpu.VMEM((hidden, w), BF16) for _, w in out_pieces],
             pltpu.VMEM((batch, d), BF16),
             pltpu.VMEM((batch * heads, head), F32),
             pltpu.VMEM((batch * heads, head), F32),
@@ -327,20 +339,22 @@
             pltpu.VMEM((batch, d), BF16),
             pltpu.VMEM((batch, hidden), BF16),
             [pltpu.VMEM((n, count, d), BF16) for _, count in chunks],
-            pltpu.VMEM((n - 1, batch, block), BF16),
-            pltpu.VMEM((n - 1, batch, block), BF16),
-            pltpu.VMEM((n, batch, block), BF16),
+            [pltpu.VMEM((batch, w), F32) for _, w in out_pieces],
+            [pltpu.VMEM((n, batch, w // n), BF16) for _, w in out_pieces],
+            [pltpu.VMEM((n - 1, batch, w // n), BF16) for _, w in out_pieces],
+            [pltpu.VMEM((batch, w), BF16) for _, w in out_pieces],
             dma(()), dma((3,)), dma((DEPTH,)), dma((DEPTH,)), dma((len(q_pieces),)), dma(()),
-            dma((len(hidden_pieces),)), dma((len(hidden_pieces),)), dma((n,)), dma((n,)),
-            dma((len(chunks), n - 1)), dma((len(chunks), n - 1)), dma((n - 1,)), dma((n - 1,)), dma((n - 1,)), dma((n - 1,)),
+            dma((len(hidden_pieces),)), dma((len(hidden_pieces),)), dma((len(out_pieces),)), dma(()),
+            dma((len(chunks),)), dma((len(chunks),)),
+            dma(()), dma((len(out_pieces),)), dma(()), dma((len(out_pieces),)),
         ]
         return pl.pallas_call(
-            functools.partial(layer_kernel, n, chunks, hidden_pieces, q_pieces),
+            functools.partial(layer_kernel, n, chunks, hidden_pieces, q_pieces, out_pieces),
             out_shape=jax.ShapeDtypeStruct(x.shape, x.dtype),
             in_specs=[any_space] * 11,
             out_specs=any_space,
             scratch_shapes=scratch,
-            compiler_params=pltpu.CompilerParams(collective_id=0, has_side_effects=True, vmem_limit_bytes=67043328),
+            compiler_params=pltpu.CompilerParams(collective_id=0, has_side_effects=True, vmem_limit_bytes=VMEM_BYTES),
             name="layer",
         )(x, k, v, gain_a, gain_m, jnp.asarray(rope_rows(cache - 1, head)), wq, wo, w_gate, w_up, w_down)
 

time: 112 us -> 109 us (0.973)
  Pallas kernels: 110 us -> 107 us
    pallas_call x1, Pallas kernels: 110 us -> 107 us  [step(): pl.pallas_call(functools.partial(layer_kernel, n, chunks, hidden_pieces,...]
where the time goes in v2:
time: 109 us; the launch traced here: 108 us
  Pallas kernels  107 us (98%)
  local copies, waits for them, and re-layouts  1.72 us (2%)
    pallas_call x1, Pallas kernels, step(): pl.pallas_call(functools.partial(layer_kernel, n, chunks, hidden_pieces,...  107 us

profile of v2, /device:TPU:112, one launch (start us, length us, event | category | flops | bytes accessed | tf_op | source)
XLA Modules:
  0.0 108.4 jit_solution(7297448694429213955)
XLA Ops:
  0.0 106.7 %layer.1 = bf16[64,2560]{1,0:T(8,128)(2,1)} custom-call(bf16[64,2560]{1,0:T(8,128)(2,1)} %x_hbm.1, bf16[64,2,4096,128]{3,2,1,0:T(8,128)(2,1)} %bitcast.k_hbm, bf16[64,2,4096,128]{3,2,1,0:T(8,128)(2,1)} %bitcast.1.v_hbm, bf16[2560]{0:T(1024)(128)(2,1)} %gain_a_hbm.1, bf16[2560]{0:T(1024)(128)(2,1)} %gain_m_hbm.1, f32[2,128]{1,0:T(2,128)} %constant.2.clone.rope_hbm, ...), custom_call_target="tpu_custom_call" | custom-call | tf_op jit(solution)/shard_map/layer/pallas_call | solution.py:351
  106.7 1.7 %copy.13 = bf16[64,2560]{1,0:T(8,128)(2,1)} copy(bf16[64,2560]{1,0:T(8,128)(2,1)} %layer.1) | data formatting | bytes 655360

commit v3 on v2

--- a/solution.py
+++ b/solution.py
@@ -17,6 +17,7 @@
 MESH = pl.DeviceIdType.MESH
 F32, BF16 = jnp.float32, jnp.bfloat16
 EPS = 1e-6
+STEPS = (((0, 1, 2), ()), ((3, 4), (0,)), ((), (1, 2)), ((), (3, 4)))
 
 
 def dot(a, b):
@@ -230,7 +231,6 @@
         project(c, first, count)
 
     ahead = len(streamed) - 9
-    out_groups = [(0, 1), (2, 3, 4)]
     for j in range(ahead):
         streamed[j].wait()
         stream(9 + j, 1)
@@ -246,14 +246,6 @@
             h_ref[at : at + 8, :] = h
             b_ref[at : at + 8, :] = normed(h.astype(F32), gain_m)
 
-    for start, upto in ((0, 3), (3, len(hidden_pieces))):
-        for c in streamed[max(ahead, 2 * start) : 2 * upto]:
-            c.wait()
-        for j, (at, w) in list(enumerate(hidden_pieces))[start:upto]:
-            gate = dot(b_ref[...], wg_refs[j][...])
-            up = dot(b_ref[...], wu_refs[j][...])
-            hid_ref[:, at : at + w] = (gate / (1.0 + jnp.exp(-gate)) * up).astype(BF16)
-
     def share(at, w):
         return pl.ds(pl.multiple_of(at + me * (w // n), LANES), w // n)
 
@@ -273,10 +265,18 @@
         at, w = out_pieces[p]
         return pltpu.make_async_copy(y_refs[p], out_hbm.at[:, pl.ds(at, w)], out_sem)
 
-    for group in out_groups:
-        for p in group:
-            copies_wd[p].wait()
-        for p in group:
+    arrived = ahead
+    for inner, outer in STEPS:
+        upto = 2 * len(hidden_pieces) + outer[-1] + 1 if outer else 2 * inner[-1] + 2
+        for c in streamed[arrived:upto]:
+            c.wait()
+        arrived = max(arrived, upto)
+        for j in inner:
+            at, w = hidden_pieces[j]
+            gate = dot(b_ref[...], wg_refs[j][...])
+            up = dot(b_ref[...], wu_refs[j][...])
+            hid_ref[:, at : at + w] = (gate / (1.0 + jnp.exp(-gate)) * up).astype(BF16)
+        for p in outer:
             term = dot(hid_ref[...], wd_refs[p][...])
             own_refs[p][...] = term
             width = out_pieces[p][1] // n

time: 109 us -> 108 us (level)
  no operation moved by 1% of the time
where the time goes in v3:
time: 108 us
  Pallas kernels  107 us (99%)
  local copies, waits for them, and re-layouts  1.72 us (2%)
    pallas_call x1, Pallas kernels, step(): pl.pallas_call(functools.partial(layer_kernel, n, chunks, hidden_pieces,...  107 us

profile of v3, /device:TPU:112, one launch (start us, length us, event | category | flops | bytes accessed | tf_op | source)
XLA Modules:
  0.0 108.3 jit_solution(11617054121042256541)
XLA Ops:
  0.0 106.5 %layer.1 = bf16[64,2560]{1,0:T(8,128)(2,1)} custom-call(bf16[64,2560]{1,0:T(8,128)(2,1)} %x_hbm.1, bf16[64,2,4096,128]{3,2,1,0:T(8,128)(2,1)} %bitcast.k_hbm, bf16[64,2,4096,128]{3,2,1,0:T(8,128)(2,1)} %bitcast.1.v_hbm, bf16[2560]{0:T(1024)(128)(2,1)} %gain_a_hbm.1, bf16[2560]{0:T(1024)(128)(2,1)} %gain_m_hbm.1, f32[2,128]{1,0:T(2,128)} %constant.2.clone.rope_hbm, ...), custom_call_target="tpu_custom_call" | custom-call | tf_op jit(solution)/shard_map/layer/pallas_call | solution.py:351
  106.6 1.7 %copy.13 = bf16[64,2560]{1,0:T(8,128)(2,1)} copy(bf16[64,2560]{1,0:T(8,128)(2,1)} %layer.1) | data formatting | bytes 655360
